TPU v7x, 32 devices: a whole 2x2x4 slice. The times are simulated.
32 devices in a mesh: dp: 8 (over y, x, core), seq: 4 (over z).
Axes of the slice: x: 2, y: 2, z: 4, core: 2. Of those that a mesh axis runs over, the one named last changes fastest.
Arguments:
- student_in: bfloat16 [4096, 3584], P(('dp', 'seq')), may hold values from -6 to 6
- weight: bfloat16 [3584, 512], P(('dp', 'seq')), may hold values from -0.09375 to 0.09375
- queries: bfloat16 [4096, 512], P(('dp', 'seq')), may hold values from -8 to 8, as said below
- keys: bfloat16 [4096, 128], P(('dp', 'seq')), may hold values from -8 to 8
- values: bfloat16 [4096, 128], P(('dp', 'seq')), may hold values from -6 to 6
- lengths: int32 [8, 4], P('dp'), may hold values from 1 to 384, 512 in all within a row
- assignment: int32 [8, 4], P('dp'), may hold values from 0 to 3, each once within a row
Outputs:
- attention: bfloat16 [4096, 512], P(('dp', 'seq'))
- weight_grad: float32 [3584, 512], P(('dp', 'seq'))
Inputs may be any that keep to these rules, and one draw needn't show every extreme that they name: `queries`: entries of head 0 and of keys may reach the ends of this range. Each row holds the lengths of 4 rollouts of one sequence, summing to 512, the longest exactly 384. `assignment`: each row is a permutation of the 4 rollout blocks of one sequence.
All inputs are finite; a program needn't handle non-finite values.
Results may differ from a plain program's by a relative error of at most 0.012.
Values may be sent and summed in bfloat16 or wider, within the bound.
A program may use at most 64 MiB of HBM per device.

v0:
```python
import functools
import math

import jax
import jax.numpy as jnp
from jax import lax
from jax.experimental import pallas as pl
from jax.experimental.pallas import tpu as pltpu
from jax.sharding import PartitionSpec as P

HD = 128
HQ = 4
BLK = 128


EPSILON = 1e-06
NEGATIVE = -1e30


def locate(assign_row, doc_ends, first_slot, count):
    slot_ids = first_slot + jnp.arange(count, dtype=jnp.int32)
    block_ids = slot_ids // BLK
    block_table = jnp.arange(assign_row.shape[0], dtype=jnp.int32)
    placed = jnp.sum(
        jnp.where(block_ids[:, None] == block_table[None, :], assign_row[None, :], 0), axis=1
    )
    position = placed * BLK + slot_ids % BLK
    document = jnp.sum((position[:, None] >= doc_ends[None, :]).astype(jnp.int32), axis=1)
    return (position, document)


def absorb_block(state, key_block, value_block, query_heads, allowed):
    run_max, run_total, run_acc = state
    scores = jnp.einsum(
        "qhd,kd->hqk", query_heads, key_block, preferred_element_type=jnp.float32
    ) * HD ** (-0.5)
    masked = jnp.where(allowed[None], scores, NEGATIVE)
    new_max = jnp.maximum(run_max, jnp.max(masked, axis=-1))
    fading = jnp.exp(run_max - new_max)
    exp_terms = jnp.where(allowed[None], jnp.exp(masked - new_max[:, :, None]), 0.0)
    new_total = run_total * fading + jnp.sum(exp_terms, axis=-1)
    mixture = jnp.einsum(
        "hqk,kd->qhd",
        exp_terms.astype(jnp.bfloat16),
        value_block,
        preferred_element_type=jnp.float32,
    )
    new_acc = run_acc * fading.T[:, :, None] + mixture
    return (new_max, new_total, new_acc)


def local(student_in, weight, queries, keys, values, lengths, assignment):
    rows = queries.shape[0]
    assign_row = assignment[0]
    doc_ends = jnp.cumsum(lengths[0])
    query_pos, query_doc = locate(assign_row, doc_ends, lax.axis_index("seq") * rows, rows)
    query_heads = queries.reshape(rows, HQ, HD)
    start_state = (
        jnp.full((HQ, rows), NEGATIVE, jnp.float32),
        jnp.zeros((HQ, rows), jnp.float32),
        jnp.zeros((rows, HQ, HD), jnp.float32),
    )
    key_piece = lax.all_gather(keys, "seq", axis=0, tiled=True)
    value_piece = lax.all_gather(values, "seq", axis=0, tiled=True)
    count = key_piece.shape[0]
    step_rows = math.gcd(count, 512)
    steps_count = count // step_rows
    key_pos, key_doc = locate(assign_row, doc_ends, jnp.int32(0), count)

    def one_step(running, slabs):
        key_block, value_block, key_position, key_document = slabs
        allowed = (query_doc[:, None] == key_document[None, :]) & (
            query_pos[:, None] >= key_position[None, :]
        )
        updated = absorb_block(running, key_block, value_block, query_heads, allowed)
        return (updated, None)

    slabs = (
        key_piece.reshape(steps_count, step_rows, HD),
        value_piece.reshape(steps_count, step_rows, HD),
        key_pos.reshape(steps_count, step_rows),
        key_doc.reshape(steps_count, step_rows),
    )
    result, _ = lax.scan(one_step, start_state, slabs)
    final_max, final_total, final_acc = result
    attention = (final_acc / final_total.T[:, :, None]).reshape(rows, HQ * HD).astype(jnp.bfloat16)
    as_float = student_in.astype(jnp.float32)
    normed = (
        as_float * lax.rsqrt(jnp.mean(as_float * as_float, axis=1, keepdims=True) + EPSILON)
    ).astype(jnp.bfloat16)
    group_rows = lax.all_gather(weight, "seq", axis=0, tiled=True)
    columns = normed
    predicted = jnp.dot(
        columns,
        lax.all_gather(group_rows, "dp", axis=0, tiled=True),
        preferred_element_type=jnp.float32,
    )
    dp_count = lax.axis_size("dp")
    seq_count = lax.axis_size("seq")
    token_total = rows * dp_count * seq_count
    scaled = ((predicted - attention.astype(jnp.float32)) * token_total ** (-0.5)).astype(
        jnp.bfloat16
    )
    columns = normed
    outer_rows = lax.psum_scatter(
        lax.dot_general(
            columns, scaled, (((0,), (0,)), ((), ())), preferred_element_type=jnp.float32
        ).astype(jnp.bfloat16),
        "dp",
        scatter_dimension=0,
        tiled=True,
    )
    weight_grad = lax.psum_scatter(outer_rows, "seq", scatter_dimension=0, tiled=True).astype(
        jnp.float32
    )
    return (attention, weight_grad)


MESH = pl.DeviceIdType.MESH
F32 = jnp.float32
BF16 = jnp.bfloat16


def fused_kernel(
    token_total,
    x_ref, w_ref, q_ref, k_ref, v_ref, len_ref, asg_ref,
    att_ref, out_ref,
    xs, xt, w_all, kv_all, inv, pred, p_out, p_in, s_all, att_half, att_peer,
    grad_f, s_y, r_y, s_z, r_z,
    send, send_z, sem_w, sem_kv, sem_x, sem_inv, sem_att, sem_p, sem_s, sem_ry, sem_rz,
):
    rows = q_ref.shape[0]
    piece = w_ref.shape[0]
    half = w_ref.shape[1] // 2
    depth = xs.shape[3]
    dp, z = lax.axis_index("dp"), lax.axis_index("seq")
    c = dp % 2
    pc = 1 - c
    x = (dp // 2) % 2
    y = dp // 4
    yo = 1 - y
    mate = (dp + 1 - 2 * c, z)
    xn_dev = (dp + 2 - 4 * x, z)
    yn_dev = (dp + 4 - 8 * y, z)
    zs = (z, z + 1 - 2 * (z % 2), z + 2 - 4 * (z // 2), 3 - z)
    z_dev = [(dp, zs[r]) for r in range(4)]
    z_mate = [(dp + 1 - 2 * c, zs[r]) for r in range(4)]

    below, above = (dp, (z + 3) % 4), (dp, (z + 1) % 4)
    barrier = pltpu.get_barrier_semaphore()
    for dev in (mate, xn_dev, yn_dev):
        pl.semaphore_signal(barrier, inc=1, device_id=dev, device_id_type=MESH)
    for present, dev in ((z > 0, below), (z < 3, above)):

        @pl.when(present)
        def _():
            pl.semaphore_signal(barrier, inc=1, device_id=dev, device_id_type=MESH)

    pl.semaphore_wait(barrier, 3 + jnp.minimum(z, 1) + jnp.minimum(3 - z, 1))

    sent = []
    sent_when = []

    def push_when(present, src, dst, rsem, dev):
        copy = pltpu.make_async_remote_copy(
            src_ref=src, dst_ref=dst, send_sem=send_z.at[len(sent_when)], recv_sem=rsem,
            device_id=dev, device_id_type=MESH,
        )
        pl.when(present)(copy.start)
        sent_when.append((present, copy))

    def both_ways(src, dst, rsem):
        push_when(z > 0, src, dst, rsem, below)
        push_when(z < 3, src, dst, rsem, above)

    def push(src, dst, rsem, dev):
        copy = pltpu.make_async_remote_copy(
            src_ref=src, dst_ref=dst, send_sem=send.at[len(sent)], recv_sem=rsem,
            device_id=dev, device_id_type=MESH,
        )
        copy.start()
        sent.append(copy)

    def arrive(dst, rsem):
        pltpu.make_async_remote_copy(
            src_ref=dst, dst_ref=dst, send_sem=send.at[0], recv_sem=rsem,
            device_id=mate, device_id_type=MESH,
        ).wait_recv()

    def cols(core):
        return pl.ds(pl.multiple_of(core * half, 128), half)

    def width(at_y, at_x):
        return pl.ds(pl.multiple_of((at_y * 2 + at_x) * depth, 128), depth)

    def w_push(at, dev):
        push(w_all.at[at], w_all.at[at], sem_w.at[at], dev)

    def w_arrive(at):
        arrive(w_all.at[at], sem_w.at[at])

    def x_push(at_y, at_x, slot, dev):
        push(x_ref.at[:, width(at_y, at_x)], xs.at[at_y, slot], sem_x.at[at_y, slot], dev)

    mine, other = (y, c, z), (y, pc, z)
    own_half = w_ref.at[:, cols(c)]
    push(w_ref.at[:, cols(pc)], w_all.at[mine], sem_w.at[mine], mate)
    both_ways(own_half, w_all.at[mine], sem_w.at[mine])
    push(own_half, w_all.at[mine], sem_w.at[mine], yn_dev)
    x_push(y, 1 - x, 2, xn_dev)
    x_push(yo, 1 - x, 2, xn_dev)
    x_push(y, x, 1, mate)
    x_push(yo, x, 1, mate)
    w_all[mine] = w_ref[:, cols(c)]
    w_arrive(other)
    both_ways(w_all.at[other], w_all.at[other], sem_w.at[other])
    w_push(other, yn_dev)
    kv_all[0, z] = k_ref[...]
    kv_all[1, z] = v_ref[...]
    xs[y, 0] = x_ref[:, width(y, x)]
    xs[yo, 0] = x_ref[:, width(yo, x)]

    step = 16

    @pl.loop(0, rows // step)
    def _(i):
        at = pl.ds(pl.multiple_of(i * step, step), step)
        block = x_ref[at, :].astype(F32)
        factor = lax.rsqrt(jnp.mean(block * block, axis=1, keepdims=True) + EPSILON)
        inv[0, at, :] = jnp.broadcast_to(factor, (step, 128))

    push(inv.at[0], inv.at[1], sem_inv.at[0], mate)

    def sources(k):
        return (
            (z >= k, (z >= k) & (z < 3), (z + 4 - k) % 4, above),
            (z + k <= 3, (z + k <= 3) & (z > 0), (z + k) % 4, below),
        )

    def forward(k):
        for part in range(2):
            for present, onward, chunk, dev in sources(k):
                at = (y, part, chunk)

                @pl.when(present)
                def _():
                    w_arrive(at)

                if k < 3:
                    push_when(onward, w_all.at[at], w_all.at[at], sem_w.at[at], dev)
                push_when(present, w_all.at[at], w_all.at[at], sem_w.at[at], yn_dev)

    def kv_forward(k):
        for part in range(2):
            for present, onward, chunk, dev in sources(k):
                at = (part, chunk)

                @pl.when(present)
                def _():
                    arrive(kv_all.at[at], sem_kv.at[at])

                if k < 3:
                    push_when(onward, kv_all.at[at], kv_all.at[at], sem_kv.at[at], dev)

    def x_arrive(at_y, slot):
        arrive(xs.at[at_y, slot], sem_x.at[at_y, slot])

    def x_relay(at_y):
        x_arrive(at_y, 2)
        push(xs.at[at_y, 2], xs.at[at_y, 3], sem_x.at[at_y, 3], mate)

    def turn(at_y, slot):
        for j in range(depth // 128):
            at = slice(j * 128, (j + 1) * 128)
            xt[at_y, at, slot * rows : (slot + 1) * rows] = xs[at_y, slot, :, at].T

    def w_block(at_y):
        return w_all[at_y].reshape(depth, half)

    def product(at_y, first):
        return jnp.dot(
            xs[at_y, first : first + 2].reshape(2 * rows, depth), w_block(at_y),
            preferred_element_type=F32,
        )

    forward(1)
    both_ways(k_ref, kv_all.at[0, z], sem_kv.at[0, z])
    both_ways(v_ref, kv_all.at[1, z], sem_kv.at[1, z])
    x_arrive(y, 1)
    x_arrive(yo, 1)
    for slot in range(2):

        @pl.loop(0, 2)
        def _(at_y):
            turn(at_y, slot)

    forward(2)
    x_relay(y)
    kv_forward(1)
    forward(3)
    kv_forward(2)
    pred[0] = product(y, 0)
    x_relay(yo)
    x_arrive(y, 3)
    pred[1] = product(y, 2)
    turn(y, 2)
    turn(y, 3)
    x_arrive(yo, 3)
    for r in range(4):
        for part in range(2):
            w_arrive((yo, part, zs[r]))
    p_out[...] = (pred[1] + product(yo, 2)).astype(BF16).reshape(2, rows, half)
    for slot in range(2):
        push(p_out.at[slot], p_in.at[slot], sem_p.at[slot], xn_dev)
    pred[0] += product(yo, 0)

    kv_forward(3)
    ends = []
    total = 0
    for i in range(len_ref.shape[1]):
        total = total + len_ref[0, i]
        ends.append(total)

    def document(position):
        found = jnp.zeros(position.shape, jnp.int32)
        for end in ends:
            found = found + (position >= end).astype(jnp.int32)
        return found

    lanes = lax.broadcasted_iota(jnp.int32, (1, BLK), 1)
    k_pos = jnp.concatenate([asg_ref[0, j] * BLK + lanes for j in range(4)], axis=1)
    q_pos = asg_ref[0, z] * BLK + lax.broadcasted_iota(jnp.int32, (rows, 1), 0)
    allowed = (document(q_pos) == document(k_pos)) & (q_pos >= k_pos)
    k_all = kv_all[0].reshape(4 * rows, HD)
    v_all = kv_all[1].reshape(4 * rows, HD)
    for h in range(HQ):
        scores = lax.dot_general(
            q_ref[:, h * HD : (h + 1) * HD], k_all, (((1,), (1,)), ((), ())),
            preferred_element_type=F32,
        ) * HD ** (-0.5)
        masked = jnp.where(allowed, scores, NEGATIVE)
        top = jnp.max(masked, axis=1, keepdims=True)
        terms = jnp.where(allowed, jnp.exp(masked - top), 0.0)
        totals = jnp.sum(terms, axis=1, keepdims=True)
        mixture = jnp.dot(terms.astype(BF16), v_all, preferred_element_type=F32)
        done = (mixture / totals).astype(BF16)
        att_ref[:, h * HD : (h + 1) * HD] = done
        place = (h % 2) * HD
        att_half[h // 2, :, place : place + HD] = done
    push(att_half.at[pc], att_peer, sem_att.at[0], mate)

    def scale_rows(slot, attended):
        arrive(p_in.at[slot], sem_p.at[slot])
        factor = jnp.concatenate([inv[slot]] * (half // 128), axis=1)
        raw = pred[0, slot * rows : (slot + 1) * rows, :] + p_in[slot].astype(F32)
        gap = raw * factor - attended.astype(F32)
        s_all[slot] = (gap * token_total ** (-0.5) * factor).astype(BF16)
        push(s_all.at[slot], s_all.at[slot + 2], sem_s.at[slot], xn_dev)

    scale_rows(0, att_half[c])
    arrive(att_peer, sem_att.at[0])
    arrive(inv.at[1], sem_inv.at[0])
    scale_rows(1, att_peer[...])
    turn(yo, 2)
    turn(yo, 3)

    def grad(at_y, first):
        return jnp.dot(
            xt[at_y, :, first * rows : (first + 2) * rows],
            s_all[first : first + 2].reshape(2 * rows, half),
            preferred_element_type=F32,
        ).reshape(2, 4, piece, half)

    grad_f[yo] = grad(yo, 0)
    grad_f[y] = grad(y, 0)
    for slot in range(2):
        arrive(s_all.at[slot + 2], sem_s.at[slot])
    s_y[...] = (grad_f[yo] + grad(yo, 2)).astype(BF16)
    order = (3, 2, 1, 0)
    for r in order:
        for part in range(2):
            at = (part, zs[r])
            push(s_y.at[at], r_y.at[at], sem_ry.at[at], yn_dev)
    grad_f[y] += grad(y, 2)

    def column_sum(part, g):
        arrive(r_y.at[part, g], sem_ry.at[part, g])
        return grad_f[y, part, g] + r_y[part, g].astype(F32)

    for r in order[:3]:
        g = zs[r]
        for part in range(2):
            s_z[part, g] = column_sum(part, g).astype(BF16)
        push(s_z.at[c, g], r_z.at[z, c], sem_rz.at[z, c], z_dev[r])
        push(s_z.at[pc, g], r_z.at[z, c], sem_rz.at[z, c], z_mate[r])
    for part in range(2):
        grad_f[y, part, z] = column_sum(part, z)
    s_z[pc, z] = grad_f[y, pc, z].astype(BF16)
    push(s_z.at[pc, z], r_z.at[z, c], sem_rz.at[z, c], mate)
    total = grad_f[y, c, z]
    for r in range(1, 4):
        arrive(r_z.at[zs[r], c], sem_rz.at[zs[r], c])
        total = total + r_z[zs[r], c].astype(F32)
    out_ref[:, cols(c)] = total
    total = jnp.zeros((piece, half), F32)
    for r in (3, 2, 1, 0):
        arrive(r_z.at[zs[r], pc], sem_rz.at[zs[r], pc])
        total = total + r_z[zs[r], pc].astype(F32)
    out_ref[:, cols(pc)] = total
    for copy in sent:
        copy.wait_send()
    for present, copy in sent_when:
        pl.when(present)(copy.wait_send)


def local_fused(student_in, weight, queries, keys, values, lengths, assignment):
    rows, width = student_in.shape
    piece, features = weight.shape
    half = features // 2
    depth = width // 4
    token_total = rows * lax.axis_size("dp") * lax.axis_size("seq")
    vmem = pl.BlockSpec(memory_space=pltpu.VMEM)
    smem = pl.BlockSpec(memory_space=pltpu.SMEM)
    dma = pltpu.SemaphoreType.DMA
    quarter = (2, 4, piece, half)
    return pl.pallas_call(
        functools.partial(fused_kernel, token_total),
        out_shape=(
            jax.ShapeDtypeStruct((rows, features), BF16),
            jax.ShapeDtypeStruct((piece, features), F32),
        ),
        in_specs=[vmem] * 5 + [smem] * 2,
        out_specs=(vmem, vmem),
        scratch_shapes=[
            pltpu.VMEM((2, 4, rows, depth), BF16),
            pltpu.VMEM((2, depth, 4 * rows), BF16),
            pltpu.VMEM((2,) + quarter, BF16),
            pltpu.VMEM((2, 4, rows, HD), BF16),
            pltpu.VMEM((2, rows, 128), F32),
            pltpu.VMEM((2, 2 * rows, half), F32),
            pltpu.VMEM((2, rows, half), BF16),
            pltpu.VMEM((2, rows, half), BF16),
            pltpu.VMEM((4, rows, half), BF16),
            pltpu.VMEM((2, rows, half), BF16),
            pltpu.VMEM((rows, half), BF16),
            pltpu.VMEM((2,) + quarter, F32),
            pltpu.VMEM(quarter, BF16),
            pltpu.VMEM(quarter, BF16),
            pltpu.VMEM(quarter, BF16),
            pltpu.VMEM((4, 2, piece, half), BF16),
            dma((64,)),
            dma((64,)),
            dma((2, 2, 4)),
            dma((2, 4)),
            dma((2, 4)),
            dma((1,)),
            dma((1,)),
            dma((2,)),
            dma((2,)),
            dma((2, 4)),
            dma((4, 2)),
        ],
        compiler_params=pltpu.CompilerParams(collective_id=0, has_side_effects=True),
        name="distill",
    )(student_in, weight, queries, keys, values, lengths, assignment)


def fits(student_in, weight, queries, keys, values, lengths, assignment):
    rows, width = student_in.shape
    piece, features = weight.shape
    return (
        lax.axis_size("dp") == 8
        and lax.axis_size("seq") == 4
        and rows == BLK
        and assignment.shape[1] == 4
        and piece % 16 == 0
        and width == 32 * piece
        and width % 512 == 0
        and features == HQ * HD
        and keys.shape[1] == HD
    )


def dispatch(*arrays):
    return local_fused(*arrays) if fits(*arrays) else local(*arrays)


def solution(mesh):
    placed = (
        P(("dp", "seq"), None),
        P(("dp", "seq"), None),
        P(("dp", "seq"), None),
        P(("dp", "seq"), None),
        P(("dp", "seq"), None),
        P("dp", None),
        P("dp", None),
    )
    return jax.shard_map(
        dispatch,
        mesh=mesh,
        in_specs=placed,
        out_specs=(P(("dp", "seq"), None), P(("dp", "seq"), None)),
        check_vma=False,
    )
```

profile of v0, /device:TPU:0, one launch (start us, length us, event | category | flops | bytes accessed | tf_op | source)
XLA Modules:
  0.0 48.9 jit_solution(2984593888762066464)
XLA Ops:
  0.6 45.9 %distill.1 = (bf16[128,512]{1,0:T(8,128)(2,1)}, f32[112,512]{1,0:T(8,128)}) custom-call(bf16[128,3584]{1,0:T(8,128)(2,1)} %x_ref.1, bf16[112,512]{1,0:T(8,128)(2,1)} %w_ref.1, bf16[128,512]{1,0:T(8,128)(2,1)} %q_ref.1, bf16[128,128]{1,0:T(8,128)(2,1)} %k_ref.1, bf16[128,128]{1,0:T(8,128)(2,1)} %v_ref.1, s32[1,4]{1,0:T(1,128)} %len_ref.1, s32[1,4]{1,0:T(1,128)} %asg_ref.1), custom_call_target="tpu_custom_call" | custom-call | tf_op jit(solution)/shard_map/distill/pallas_call | solution.py:426
  46.6 0.0 copy-start
  46.6 1.6 %copy.11 = bf16[128,512]{1,0:T(8,128)(2,1)} copy(bf16[128,512]{1,0:T(8,128)(2,1)} %get-tuple-element.4) | data formatting | bytes 262144
  48.2 0.0 copy-done
  48.2 0.7 %copy.12 = f32[112,512]{1,0:T(8,128)} copy(f32[112,512]{1,0:T(8,128)S(1)} %copy-done) | data formatting | bytes 458752
Async XLA Ops:
  46.6 1.6 %copy-start = (f32[112,512]{1,0:T(8,128)S(1)}, f32[112,512]{1,0:T(8,128)}, u32[]{:S(2)}) copy-start(f32[112,512]{1,0:T(8,128)} %get-tuple-element.5) | copy-start | bytes 688132
where the time goes:
time: 49 us; the launch traced here: 48.9 us
  Pallas kernels  45.9 us (94%)
  local copies, waits for them, and re-layouts  2.3 us (5%)
  between operations  0.65 us (1%)
    pallas_call x1, Pallas kernels, local_fused(): pl.pallas_call(functools.partial(fused_kernel, token_total), out_shape=(j...  45.9 us
    unnamed x4, local copies, waits for them, and re-layouts  2.3 us

commit v1 on v0

--- a/solution.py
+++ b/solution.py
@@ -132,6 +132,7 @@
     rows = q_ref.shape[0]
     piece = w_ref.shape[0]
     half = w_ref.shape[1] // 2
+    chunk = half // 2
     depth = xs.shape[3]
     dp, z = lax.axis_index("dp"), lax.axis_index("seq")
     c = dp % 2
@@ -139,24 +140,28 @@
     x = (dp // 2) % 2
     y = dp // 4
     yo = 1 - y
-    mate = (dp + 1 - 2 * c, z)
+    dp_m = dp + 1 - 2 * c
+    mate = (dp_m, z)
     xn_dev = (dp + 2 - 4 * x, z)
     yn_dev = (dp + 4 - 8 * y, z)
+    yn_mate = (dp_m + 4 - 8 * y, z)
     zs = (z, z + 1 - 2 * (z % 2), z + 2 - 4 * (z // 2), 3 - z)
     z_dev = [(dp, zs[r]) for r in range(4)]
-    z_mate = [(dp + 1 - 2 * c, zs[r]) for r in range(4)]
-
+    z_mate = [(dp_m, zs[r]) for r in range(4)]
     below, above = (dp, (z + 3) % 4), (dp, (z + 1) % 4)
+    below_m, above_m = (dp_m, (z + 3) % 4), (dp_m, (z + 1) % 4)
+
     barrier = pltpu.get_barrier_semaphore()
-    for dev in (mate, xn_dev, yn_dev):
+    for dev in (mate, xn_dev, yn_dev, yn_mate):
         pl.semaphore_signal(barrier, inc=1, device_id=dev, device_id_type=MESH)
-    for present, dev in ((z > 0, below), (z < 3, above)):
+    for present, pair in ((z > 0, (below, below_m)), (z < 3, (above, above_m))):
 
         @pl.when(present)
         def _():
-            pl.semaphore_signal(barrier, inc=1, device_id=dev, device_id_type=MESH)
-
-    pl.semaphore_wait(barrier, 3 + jnp.minimum(z, 1) + jnp.minimum(3 - z, 1))
+            for dev in pair:
+                pl.semaphore_signal(barrier, inc=1, device_id=dev, device_id_type=MESH)
+
+    pl.semaphore_wait(barrier, 4 + 2 * (jnp.minimum(z, 1) + jnp.minimum(3 - z, 1)))
 
     sent = []
     sent_when = []
@@ -169,9 +174,9 @@
         pl.when(present)(copy.start)
         sent_when.append((present, copy))
 
-    def both_ways(src, dst, rsem):
-        push_when(z > 0, src, dst, rsem, below)
-        push_when(z < 3, src, dst, rsem, above)
+    def both_ways(src, dst, rsem, down, up):
+        push_when(z > 0, src, dst, rsem, down)
+        push_when(z < 3, src, dst, rsem, up)
 
     def push(src, dst, rsem, dev):
         copy = pltpu.make_async_remote_copy(
@@ -187,34 +192,38 @@
             device_id=mate, device_id_type=MESH,
         ).wait_recv()
 
-    def cols(core):
-        return pl.ds(pl.multiple_of(core * half, 128), half)
+    def cols(core, j):
+        return pl.ds(pl.multiple_of(core * half + j * chunk, 128), chunk)
 
     def width(at_y, at_x):
         return pl.ds(pl.multiple_of((at_y * 2 + at_x) * depth, 128), depth)
 
-    def w_push(at, dev):
-        push(w_all.at[at], w_all.at[at], sem_w.at[at], dev)
-
     def w_arrive(at):
         arrive(w_all.at[at], sem_w.at[at])
 
     def x_push(at_y, at_x, slot, dev):
         push(x_ref.at[:, width(at_y, at_x)], xs.at[at_y, slot], sem_x.at[at_y, slot], dev)
 
-    mine, other = (y, c, z), (y, pc, z)
-    own_half = w_ref.at[:, cols(c)]
-    push(w_ref.at[:, cols(pc)], w_all.at[mine], sem_w.at[mine], mate)
-    both_ways(own_half, w_all.at[mine], sem_w.at[mine])
-    push(own_half, w_all.at[mine], sem_w.at[mine], yn_dev)
+    def w_start(j):
+        at = (j, y, c, z)
+        dst, sem = w_all.at[at], sem_w.at[at]
+        own, peer = w_ref.at[:, cols(c, j)], w_ref.at[:, cols(pc, j)]
+        both_ways(own, dst, sem, below, above)
+        push(own, dst, sem, yn_dev)
+        both_ways(peer, dst, sem, below_m, above_m)
+        push(peer, dst, sem, yn_mate)
+        push(peer, dst, sem, mate)
+
+    w_start(0)
     x_push(y, 1 - x, 2, xn_dev)
     x_push(yo, 1 - x, 2, xn_dev)
+    w_start(1)
+    both_ways(k_ref, kv_all.at[0, z], sem_kv.at[0, z], below, above)
+    both_ways(v_ref, kv_all.at[1, z], sem_kv.at[1, z], below, above)
     x_push(y, x, 1, mate)
     x_push(yo, x, 1, mate)
-    w_all[mine] = w_ref[:, cols(c)]
-    w_arrive(other)
-    both_ways(w_all.at[other], w_all.at[other], sem_w.at[other])
-    w_push(other, yn_dev)
+    for j in range(2):
+        w_all[j, y, c, z] = w_ref[:, cols(c, j)]
     kv_all[0, z] = k_ref[...]
     kv_all[1, z] = v_ref[...]
     xs[y, 0] = x_ref[:, width(y, x)]
@@ -237,10 +246,10 @@
             (z + k <= 3, (z + k <= 3) & (z > 0), (z + k) % 4, below),
         )
 
-    def forward(k):
+    def forward(j, k):
         for part in range(2):
-            for present, onward, chunk, dev in sources(k):
-                at = (y, part, chunk)
+            for present, onward, at_z, dev in sources(k):
+                at = (j, y, part, at_z)
 
                 @pl.when(present)
                 def _():
@@ -252,8 +261,8 @@
 
     def kv_forward(k):
         for part in range(2):
-            for present, onward, chunk, dev in sources(k):
-                at = (part, chunk)
+            for present, onward, at_z, dev in sources(k):
+                at = (part, at_z)
 
                 @pl.when(present)
                 def _():
@@ -274,18 +283,16 @@
             at = slice(j * 128, (j + 1) * 128)
             xt[at_y, at, slot * rows : (slot + 1) * rows] = xs[at_y, slot, :, at].T
 
-    def w_block(at_y):
-        return w_all[at_y].reshape(depth, half)
-
-    def product(at_y, first):
+    def product(j, at_y, first):
         return jnp.dot(
-            xs[at_y, first : first + 2].reshape(2 * rows, depth), w_block(at_y),
+            xs[at_y, first : first + 2].reshape(2 * rows, depth),
+            w_all[j, at_y].reshape(depth, chunk),
             preferred_element_type=F32,
         )
 
-    forward(1)
-    both_ways(k_ref, kv_all.at[0, z], sem_kv.at[0, z])
-    both_ways(v_ref, kv_all.at[1, z], sem_kv.at[1, z])
+    forward(0, 1)
+    forward(1, 1)
+    kv_forward(1)
     x_arrive(y, 1)
     x_arrive(yo, 1)
     for slot in range(2):
@@ -294,27 +301,38 @@
         def _(at_y):
             turn(at_y, slot)
 
-    forward(2)
+    forward(0, 2)
+    forward(1, 2)
     x_relay(y)
-    kv_forward(1)
-    forward(3)
     kv_forward(2)
-    pred[0] = product(y, 0)
+    turn(y, 2)
+    forward(0, 3)
+    x_arrive(y, 3)
+    turn(y, 3)
+    for j in range(2):
+        w_arrive((j, y, pc, z))
+    pred[0, 0] = product(0, y, 0)
+    pred[0, 1] = product(0, y, 2)
+    forward(1, 3)
+    pred[1, 0] = product(1, y, 0)
+    pred[1, 1] = product(1, y, 2)
     x_relay(yo)
-    x_arrive(y, 3)
-    pred[1] = product(y, 2)
-    turn(y, 2)
-    turn(y, 3)
-    x_arrive(yo, 3)
-    for r in range(4):
-        for part in range(2):
-            w_arrive((yo, part, zs[r]))
-    p_out[...] = (pred[1] + product(yo, 2)).astype(BF16).reshape(2, rows, half)
-    for slot in range(2):
-        push(p_out.at[slot], p_in.at[slot], sem_p.at[slot], xn_dev)
-    pred[0] += product(yo, 0)
-
-    kv_forward(3)
+
+    def p_send(j):
+        for r in range(4):
+            for part in range(2):
+                w_arrive((j, yo, part, zs[r]))
+        if j == 0:
+            x_arrive(yo, 3)
+        p_out[j] = (pred[j, 1] + product(j, yo, 2)).astype(BF16).reshape(2, rows, chunk)
+        for slot in range(2):
+            push(p_out.at[j, slot], p_in.at[j, slot], sem_p.at[j, slot], xn_dev)
+
+    p_send(0)
+    p_send(1)
+    pred[0, 0] += product(0, yo, 0)
+    pred[1, 0] += product(1, yo, 0)
+
     ends = []
     total = 0
     for i in range(len_ref.shape[1]):
@@ -331,9 +349,11 @@
     k_pos = jnp.concatenate([asg_ref[0, j] * BLK + lanes for j in range(4)], axis=1)
     q_pos = asg_ref[0, z] * BLK + lax.broadcasted_iota(jnp.int32, (rows, 1), 0)
     allowed = (document(q_pos) == document(k_pos)) & (q_pos >= k_pos)
+    kv_forward(3)
     k_all = kv_all[0].reshape(4 * rows, HD)
     v_all = kv_all[1].reshape(4 * rows, HD)
-    for h in range(HQ):
+
+    def attend(h):
         scores = lax.dot_general(
             q_ref[:, h * HD : (h + 1) * HD], k_all, (((1,), (1,)), ((), ())),
             preferred_element_type=F32,
@@ -345,68 +365,80 @@
         mixture = jnp.dot(terms.astype(BF16), v_all, preferred_element_type=F32)
         done = (mixture / totals).astype(BF16)
         att_ref[:, h * HD : (h + 1) * HD] = done
-        place = (h % 2) * HD
-        att_half[h // 2, :, place : place + HD] = done
-    push(att_half.at[pc], att_peer, sem_att.at[0], mate)
-
-    def scale_rows(slot, attended):
-        arrive(p_in.at[slot], sem_p.at[slot])
-        factor = jnp.concatenate([inv[slot]] * (half // 128), axis=1)
-        raw = pred[0, slot * rows : (slot + 1) * rows, :] + p_in[slot].astype(F32)
+        att_half[h // 2, h % 2] = done
+
+    def scale_rows(j, slot, attended):
+        arrive(p_in.at[j, slot], sem_p.at[j, slot])
+        factor = inv[slot]
+        raw = pred[j, 0, slot * rows : (slot + 1) * rows, :] + p_in[j, slot].astype(F32)
         gap = raw * factor - attended.astype(F32)
-        s_all[slot] = (gap * token_total ** (-0.5) * factor).astype(BF16)
-        push(s_all.at[slot], s_all.at[slot + 2], sem_s.at[slot], xn_dev)
-
-    scale_rows(0, att_half[c])
-    arrive(att_peer, sem_att.at[0])
-    arrive(inv.at[1], sem_inv.at[0])
-    scale_rows(1, att_peer[...])
+        s_all[j, slot] = (gap * token_total ** (-0.5) * factor).astype(BF16)
+        push(s_all.at[j, slot], s_all.at[j, slot + 2], sem_s.at[j, slot], xn_dev)
+
+    for j in range(2):
+        attend(j)
+        attend(2 + j)
+        push(att_half.at[pc, j], att_peer.at[j], sem_att.at[j], mate)
+        scale_rows(j, 0, att_half[c, j])
+        arrive(att_peer.at[j], sem_att.at[j])
+        if j == 0:
+            arrive(inv.at[1], sem_inv.at[0])
+        scale_rows(j, 1, att_peer[j])
     turn(yo, 2)
     turn(yo, 3)
 
-    def grad(at_y, first):
+    def grad(j, at_y, first):
         return jnp.dot(
             xt[at_y, :, first * rows : (first + 2) * rows],
-            s_all[first : first + 2].reshape(2 * rows, half),
+            s_all[j, first : first + 2].reshape(2 * rows, chunk),
             preferred_element_type=F32,
-        ).reshape(2, 4, piece, half)
-
-    grad_f[yo] = grad(yo, 0)
-    grad_f[y] = grad(y, 0)
-    for slot in range(2):
-        arrive(s_all.at[slot + 2], sem_s.at[slot])
-    s_y[...] = (grad_f[yo] + grad(yo, 2)).astype(BF16)
+        ).reshape(2, 4, piece, chunk)
+
     order = (3, 2, 1, 0)
-    for r in order:
+    for j in range(2):
+        grad_f[j, 1] = grad(j, yo, 0)
+        if j == 0:
+            grad_f[0, 0] = grad(0, y, 0)
+            grad_f[1, 0] = grad(1, y, 0)
+        for slot in range(2):
+            arrive(s_all.at[j, slot + 2], sem_s.at[j, slot])
+        s_y[j] = (grad_f[j, 1] + grad(j, yo, 2)).astype(BF16)
+        for r in order:
+            for part in range(2):
+                at = (j, part, zs[r])
+                push(s_y.at[at], r_y.at[at], sem_ry.at[at], yn_dev)
+        grad_f[j, 0] += grad(j, y, 2)
+
+    def column_sum(j, part, g):
+        at = (j, part, g)
+        arrive(r_y.at[at], sem_ry.at[at])
+        return grad_f[j, 0, part, g] + r_y[at].astype(F32)
+
+    def z_push(j, part, g, dev):
+        push(s_z.at[j, part, g], r_z.at[j, z, c], sem_rz.at[j, z, c], dev)
+
+    for j in range(2):
+        for r in order[:3]:
+            g = zs[r]
+            for part in range(2):
+                s_z[j, part, g] = column_sum(j, part, g).astype(BF16)
+            z_push(j, c, g, z_dev[r])
+            z_push(j, pc, g, z_mate[r])
         for part in range(2):
-            at = (part, zs[r])
-            push(s_y.at[at], r_y.at[at], sem_ry.at[at], yn_dev)
-    grad_f[y] += grad(y, 2)
-
-    def column_sum(part, g):
-        arrive(r_y.at[part, g], sem_ry.at[part, g])
-        return grad_f[y, part, g] + r_y[part, g].astype(F32)
-
-    for r in order[:3]:
-        g = zs[r]
-        for part in range(2):
-            s_z[part, g] = column_sum(part, g).astype(BF16)
-        push(s_z.at[c, g], r_z.at[z, c], sem_rz.at[z, c], z_dev[r])
-        push(s_z.at[pc, g], r_z.at[z, c], sem_rz.at[z, c], z_mate[r])
-    for part in range(2):
-        grad_f[y, part, z] = column_sum(part, z)
-    s_z[pc, z] = grad_f[y, pc, z].astype(BF16)
-    push(s_z.at[pc, z], r_z.at[z, c], sem_rz.at[z, c], mate)
-    total = grad_f[y, c, z]
-    for r in range(1, 4):
-        arrive(r_z.at[zs[r], c], sem_rz.at[zs[r], c])
-        total = total + r_z[zs[r], c].astype(F32)
-    out_ref[:, cols(c)] = total
-    total = jnp.zeros((piece, half), F32)
-    for r in (3, 2, 1, 0):
-        arrive(r_z.at[zs[r], pc], sem_rz.at[zs[r], pc])
-        total = total + r_z[zs[r], pc].astype(F32)
-    out_ref[:, cols(pc)] = total
+            grad_f[j, 0, part, z] = column_sum(j, part, z)
+        s_z[j, pc, z] = grad_f[j, 0, pc, z].astype(BF16)
+        z_push(j, pc, z, mate)
+    for j in range(2):
+        total = grad_f[j, 0, c, z]
+        for r in range(1, 4):
+            arrive(r_z.at[j, zs[r], c], sem_rz.at[j, zs[r], c])
+            total = total + r_z[j, zs[r], c].astype(F32)
+        out_ref[:, cols(c, j)] = total
+        total = jnp.zeros((piece, chunk), F32)
+        for r in (3, 2, 1, 0):
+            arrive(r_z.at[j, zs[r], pc], sem_rz.at[j, zs[r], pc])
+            total = total + r_z[j, zs[r], pc].astype(F32)
+        out_ref[:, cols(pc, j)] = total
     for copy in sent:
         copy.wait_send()
     for present, copy in sent_when:
@@ -416,13 +448,13 @@
 def local_fused(student_in, weight, queries, keys, values, lengths, assignment):
     rows, width = student_in.shape
     piece, features = weight.shape
-    half = features // 2
+    chunk = features // 4
     depth = width // 4
     token_total = rows * lax.axis_size("dp") * lax.axis_size("seq")
     vmem = pl.BlockSpec(memory_space=pltpu.VMEM)
     smem = pl.BlockSpec(memory_space=pltpu.SMEM)
     dma = pltpu.SemaphoreType.DMA
-    quarter = (2, 4, piece, half)
+    quarter = (2, 4, piece, chunk)
     return pl.pallas_call(
         functools.partial(fused_kernel, token_total),
         out_shape=(
@@ -434,31 +466,31 @@
         scratch_shapes=[
             pltpu.VMEM((2, 4, rows, depth), BF16),
             pltpu.VMEM((2, depth, 4 * rows), BF16),
-            pltpu.VMEM((2,) + quarter, BF16),
+            pltpu.VMEM((2, 2) + quarter, BF16),
             pltpu.VMEM((2, 4, rows, HD), BF16),
             pltpu.VMEM((2, rows, 128), F32),
-            pltpu.VMEM((2, 2 * rows, half), F32),
-            pltpu.VMEM((2, rows, half), BF16),
-            pltpu.VMEM((2, rows, half), BF16),
-            pltpu.VMEM((4, rows, half), BF16),
-            pltpu.VMEM((2, rows, half), BF16),
-            pltpu.VMEM((rows, half), BF16),
-            pltpu.VMEM((2,) + quarter, F32),
-            pltpu.VMEM(quarter, BF16),
-            pltpu.VMEM(quarter, BF16),
-            pltpu.VMEM(quarter, BF16),
-            pltpu.VMEM((4, 2, piece, half), BF16),
-            dma((64,)),
-            dma((64,)),
-            dma((2, 2, 4)),
+            pltpu.VMEM((2, 2, 2 * rows, chunk), F32),
+            pltpu.VMEM((2, 2, rows, chunk), BF16),
+            pltpu.VMEM((2, 2, rows, chunk), BF16),
+            pltpu.VMEM((2, 4, rows, chunk), BF16),
+            pltpu.VMEM((2, 2, rows, chunk), BF16),
+            pltpu.VMEM((2, rows, chunk), BF16),
+            pltpu.VMEM((2, 2) + quarter, F32),
+            pltpu.VMEM((2,) + quarter, BF16),
+            pltpu.VMEM((2,) + quarter, BF16),
+            pltpu.VMEM((2,) + quarter, BF16),
+            pltpu.VMEM((2, 4, 2, piece, chunk), BF16),
+            dma((96,)),
+            dma((96,)),
+            dma((2, 2, 2, 4)),
             dma((2, 4)),
             dma((2, 4)),
             dma((1,)),
-            dma((1,)),
             dma((2,)),
-            dma((2,)),
-            dma((2, 4)),
-            dma((4, 2)),
+            dma((2, 2)),
+            dma((2, 2)),
+            dma((2, 2, 4)),
+            dma((2, 4, 2)),
         ],
         compiler_params=pltpu.CompilerParams(collective_id=0, has_side_effects=True),
         name="distill",

time: 49 us -> 47.8 us (0.976)
  Pallas kernels: 45.9 us -> 44.6 us
    pallas_call x1, Pallas kernels: 45.9 us -> 44.6 us  [local_fused(): pl.pallas_call(functools.partial(fused_kernel, token_total), out_shape=(j...]
where the time goes in v1:
time: 47.8 us; the launch traced here: 47.6 us
  Pallas kernels  44.6 us (93%)
  local copies, waits for them, and re-layouts  2.3 us (5%)
  between operations  0.65 us (1%)
    pallas_call x1, Pallas kernels, local_fused(): pl.pallas_call(functools.partial(fused_kernel, token_total), out_shape=(j...  44.6 us
    unnamed x4, local copies, waits for them, and re-layouts  2.3 us

profile of v1, /device:TPU:0, one launch (start us, length us, event | category | flops | bytes accessed | tf_op | source)
XLA Modules:
  0.0 47.6 jit_solution(844789112552656367)
XLA Ops:
  0.6 44.6 %distill.1 = (bf16[128,512]{1,0:T(8,128)(2,1)}, f32[112,512]{1,0:T(8,128)}) custom-call(bf16[128,3584]{1,0:T(8,128)(2,1)} %x_ref.1, bf16[112,512]{1,0:T(8,128)(2,1)} %w_ref.1, bf16[128,512]{1,0:T(8,128)(2,1)} %q_ref.1, bf16[128,128]{1,0:T(8,128)(2,1)} %k_ref.1, bf16[128,128]{1,0:T(8,128)(2,1)} %v_ref.1, s32[1,4]{1,0:T(1,128)} %len_ref.1, s32[1,4]{1,0:T(1,128)} %asg_ref.1), custom_call_target="tpu_custom_call" | custom-call | tf_op jit(solution)/shard_map/distill/pallas_call | solution.py:458
  45.2 0.0 copy-start
  45.3 1.6 %copy.11 = bf16[128,512]{1,0:T(8,128)(2,1)} copy(bf16[128,512]{1,0:T(8,128)(2,1)} %get-tuple-element.4) | data formatting | bytes 262144
  46.9 0.0 copy-done
  46.9 0.7 %copy.12 = f32[112,512]{1,0:T(8,128)} copy(f32[112,512]{1,0:T(8,128)S(1)} %copy-done) | data formatting | bytes 458752
Async XLA Ops:
  45.2 1.6 %copy-start = (f32[112,512]{1,0:T(8,128)S(1)}, f32[112,512]{1,0:T(8,128)}, u32[]{:S(2)}) copy-start(f32[112,512]{1,0:T(8,128)} %get-tuple-element.5) | copy-start | bytes 688132

commit v2 on v1

v2 whole, which is shorter than its diff:
```python
import functools
import math

import jax
import jax.numpy as jnp
from jax import lax
from jax.experimental import pallas as pl
from jax.experimental.pallas import tpu as pltpu
from jax.sharding import PartitionSpec as P

HD = 128
HQ = 4
BLK = 128


EPSILON = 1e-06
NEGATIVE = -1e30


def locate(assign_row, doc_ends, first_slot, count):
    slot_ids = first_slot + jnp.arange(count, dtype=jnp.int32)
    block_ids = slot_ids // BLK
    block_table = jnp.arange(assign_row.shape[0], dtype=jnp.int32)
    placed = jnp.sum(
        jnp.where(block_ids[:, None] == block_table[None, :], assign_row[None, :], 0), axis=1
    )
    position = placed * BLK + slot_ids % BLK
    document = jnp.sum((position[:, None] >= doc_ends[None, :]).astype(jnp.int32), axis=1)
    return (position, document)


def absorb_block(state, key_block, value_block, query_heads, allowed):
    run_max, run_total, run_acc = state
    scores = jnp.einsum(
        "qhd,kd->hqk", query_heads, key_block, preferred_element_type=jnp.float32
    ) * HD ** (-0.5)
    masked = jnp.where(allowed[None], scores, NEGATIVE)
    new_max = jnp.maximum(run_max, jnp.max(masked, axis=-1))
    fading = jnp.exp(run_max - new_max)
    exp_terms = jnp.where(allowed[None], jnp.exp(masked - new_max[:, :, None]), 0.0)
    new_total = run_total * fading + jnp.sum(exp_terms, axis=-1)
    mixture = jnp.einsum(
        "hqk,kd->qhd",
        exp_terms.astype(jnp.bfloat16),
        value_block,
        preferred_element_type=jnp.float32,
    )
    new_acc = run_acc * fading.T[:, :, None] + mixture
    return (new_max, new_total, new_acc)


def local(student_in, weight, queries, keys, values, lengths, assignment):
    rows = queries.shape[0]
    assign_row = assignment[0]
    doc_ends = jnp.cumsum(lengths[0])
    query_pos, query_doc = locate(assign_row, doc_ends, lax.axis_index("seq") * rows, rows)
    query_heads = queries.reshape(rows, HQ, HD)
    start_state = (
        jnp.full((HQ, rows), NEGATIVE, jnp.float32),
        jnp.zeros((HQ, rows), jnp.float32),
        jnp.zeros((rows, HQ, HD), jnp.float32),
    )
    key_piece = lax.all_gather(keys, "seq", axis=0, tiled=True)
    value_piece = lax.all_gather(values, "seq", axis=0, tiled=True)
    count = key_piece.shape[0]
    step_rows = math.gcd(count, 512)
    steps_count = count // step_rows
    key_pos, key_doc = locate(assign_row, doc_ends, jnp.int32(0), count)

    def one_step(running, slabs):
        key_block, value_block, key_position, key_document = slabs
        allowed = (query_doc[:, None] == key_document[None, :]) & (
            query_pos[:, None] >= key_position[None, :]
        )
        updated = absorb_block(running, key_block, value_block, query_heads, allowed)
        return (updated, None)

    slabs = (
        key_piece.reshape(steps_count, step_rows, HD),
        value_piece.reshape(steps_count, step_rows, HD),
        key_pos.reshape(steps_count, step_rows),
        key_doc.reshape(steps_count, step_rows),
    )
    result, _ = lax.scan(one_step, start_state, slabs)
    final_max, final_total, final_acc = result
    attention = (final_acc / final_total.T[:, :, None]).reshape(rows, HQ * HD).astype(jnp.bfloat16)
    as_float = student_in.astype(jnp.float32)
    normed = (
        as_float * lax.rsqrt(jnp.mean(as_float * as_float, axis=1, keepdims=True) + EPSILON)
    ).astype(jnp.bfloat16)
    group_rows = lax.all_gather(weight, "seq", axis=0, tiled=True)
    columns = normed
    predicted = jnp.dot(
        columns,
        lax.all_gather(group_rows, "dp", axis=0, tiled=True),
        preferred_element_type=jnp.float32,
    )
    dp_count = lax.axis_size("dp")
    seq_count = lax.axis_size("seq")
    token_total = rows * dp_count * seq_count
    scaled = ((predicted - attention.astype(jnp.float32)) * token_total ** (-0.5)).astype(
        jnp.bfloat16
    )
    columns = normed
    outer_rows = lax.psum_scatter(
        lax.dot_general(
            columns, scaled, (((0,), (0,)), ((), ())), preferred_element_type=jnp.float32
        ).astype(jnp.bfloat16),
        "dp",
        scatter_dimension=0,
        tiled=True,
    )
    weight_grad = lax.psum_scatter(outer_rows, "seq", scatter_dimension=0, tiled=True).astype(
        jnp.float32
    )
    return (attention, weight_grad)


MESH = pl.DeviceIdType.MESH
F32 = jnp.float32
BF16 = jnp.bfloat16


def fused_kernel(
    token_total,
    x_hbm, w_hbm, q_hbm, k_hbm, v_hbm, len_hbm, asg_hbm,
    att_ref, out_ref,
    xs, xo, xt, w_all, w_peer, q_ref, kv_all, len_ref, asg_ref, inv, inv_row, pred, p_out, p_in,
    s_all, att_half, att_peer, grad_f, s_y, r_y, s_z, r_z, bulk,
    local_sem, send, sem_w, sem_w_far, sem_kv, sem_x, sem_inv, sem_att, sem_p, sem_ry, sem_rz,
):
    rows = q_ref.shape[0]
    piece = w_hbm.shape[0]
    half = w_hbm.shape[1] // 2
    chunk = half // 2
    depth = xs.shape[3]
    dp, z = lax.axis_index("dp"), lax.axis_index("seq")
    c = dp % 2
    pc = 1 - c
    x = (dp // 2) % 2
    y = dp // 4
    yo = 1 - y
    dp_m = dp + 1 - 2 * c
    mate = (dp_m, z)
    xn_dev = (dp + 2 - 4 * x, z)
    xn_mate = (dp_m + 2 - 4 * x, z)
    yn_dev = (dp + 4 - 8 * y, z)
    yn_mate = (dp_m + 4 - 8 * y, z)
    zs = (z, z + 1 - 2 * (z % 2), z + 2 - 4 * (z // 2), 3 - z)
    mid = ((z + 1) // 2) % 2
    z_two = mid * zs[3] + (1 - mid) * zs[2]
    z_from = (
        mid * zs[3] + (1 - mid) * zs[1],
        mid * zs[1] + (1 - mid) * zs[2],
        mid * zs[2] + (1 - mid) * zs[3],
    )
    z_dev = [(dp, zs[r]) for r in range(4)]
    z_mate = [(dp_m, zs[r]) for r in range(4)]

    def cols(core, j):
        return pl.ds(pl.multiple_of(core * half + j * chunk, 128), chunk)

    def width(at_y, at_x):
        return pl.ds(pl.multiple_of((at_y * 2 + at_x) * depth, 128), depth)

    barrier = pltpu.get_barrier_semaphore()
    greeted = [mate, xn_dev, xn_mate, yn_dev, yn_mate] + z_dev[1:] + z_mate[1:]
    for dev in greeted:
        pl.semaphore_signal(barrier, inc=1, device_id=dev, device_id_type=MESH)

    def lines(ref):
        return math.prod(ref.shape) * jnp.dtype(ref.dtype).itemsize // 256

    def fetch(at, *pairs):
        copies = [pltpu.make_async_copy(a, b, local_sem.at[at]) for a, b in pairs]
        for copy in copies:
            copy.start()
        return sum(lines(b) for _, b in pairs)

    def amount(count, sem):
        part = bulk.at[pl.ds(0, count)]
        return pltpu.make_async_copy(part, part, sem)

    get_w = [
        fetch(
            j,
            (w_hbm.at[:, cols(c, j)], w_all.at[j, y, c, z]),
            (w_hbm.at[:, cols(pc, j)], w_peer.at[j]),
        )
        for j in range(2)
    ]
    get_xo = [
        fetch(2 + i, (x_hbm.at[:, width(at, 1 - x)], xo.at[at])) for i, at in enumerate((y, yo))
    ]
    get_kv = fetch(4, *((ref, kv_all.at[i, z]) for i, ref in enumerate((k_hbm, v_hbm))))
    get_xs = fetch(5, *((x_hbm.at[:, width(at, x)], xs.at[at, 0]) for at in (y, yo)))
    fetch(6, (q_hbm, q_ref))
    fetch(7, (len_hbm, len_ref))
    fetch(8, (asg_hbm, asg_ref))
    pl.semaphore_wait(barrier, len(greeted))

    sent = [0, 0, 0, 0, 0]

    def push(src, dst, rsem, dev, group, counted=True):
        copy = pltpu.make_async_remote_copy(
            src_ref=src, dst_ref=dst, send_sem=send.at[group], recv_sem=rsem,
            device_id=dev, device_id_type=MESH,
        )
        copy.start()
        if counted:
            sent[group] += lines(src)

    def arrive(dst, rsem):
        pltpu.make_async_remote_copy(
            src_ref=dst, dst_ref=dst, send_sem=send.at[0], recv_sem=rsem,
            device_id=mate, device_id_type=MESH,
        ).wait_recv()

    def w_start(j):
        at = (j, y, c, z)
        dst, sem = w_all.at[at], sem_w.at[j, c, z]
        amount(get_w[j], local_sem.at[j]).wait()
        push(dst, dst, sem, (dp, z_two), 0)
        push(w_peer.at[j], dst, sem, (dp_m, z_two), 0)
        push(dst, dst, sem, z_dev[1], 0)
        push(w_peer.at[j], dst, sem, z_mate[1], 0)
        push(dst, dst, sem_w_far.at[j], yn_dev, 0)
        push(w_peer.at[j], dst, sem_w_far.at[j], yn_mate, 0)
        push(w_peer.at[j], dst, sem, mate, 0)

    w_start(0)
    for i, at_y in enumerate((y, yo)):
        amount(get_xo[i], local_sem.at[2 + i]).wait()
        push(xo.at[at_y], xs.at[at_y, 2], sem_x.at[at_y, 2], xn_dev, 1)
    amount(get_kv, local_sem.at[4]).wait()
    kv_own = kv_all.at[:, z]
    push(kv_own, kv_own, sem_kv.at[z], (dp, z_two), 2)
    push(kv_own, kv_own, sem_kv.at[z], z_dev[1], 2)
    w_start(1)
    amount(get_xs, local_sem.at[5]).wait()
    push(xs.at[:, 0], xs.at[:, 1], sem_x.at[0, 1], mate, 1)

    step = 16

    @pl.loop(0, rows // step)
    def _(i):
        at = pl.ds(pl.multiple_of(i * step, step), step)
        total = jnp.zeros((step, 1), F32)
        for ref in (xs.at[0, 0], xs.at[1, 0], xo.at[0], xo.at[1]):
            block = ref[at, :].astype(F32)
            total = total + jnp.sum(block * block, axis=1, keepdims=True)
        factor = lax.rsqrt(total / (4 * depth) + EPSILON)
        inv[0, at, :] = jnp.broadcast_to(factor, (step, 128))

    inv_row[0] = inv[0].T[:8]
    push(inv_row.at[0], inv_row.at[1], sem_inv.at[0], mate, 2)
    push(inv_row.at[0], inv_row.at[2], sem_inv.at[1], xn_dev, 2)
    push(inv_row.at[0], inv_row.at[3], sem_inv.at[1], xn_mate, 2)

    relayed = []

    def relay(ref, sem, k, where):
        if k == 1 or where == 0:
            return
        copy = pltpu.make_async_remote_copy(
            src_ref=ref, dst_ref=ref, send_sem=send.at[5], recv_sem=sem,
            device_id=z_dev[1], device_id_type=MESH,
        )
        if where == 1:
            copy.start()
        else:
            pl.when(mid == 1)(copy.start)
        relayed.append(lines(ref))

    def forward(j, k, where=None):
        for part in range(2):
            at = (j, y, part, z_from[k])
            arrive(w_all.at[at], sem_w.at[j, part, z_from[k]])
            relay(w_all.at[at], sem_w.at[j, part, z_from[k]], k, where)
            push(w_all.at[at], w_all.at[at], sem_w_far.at[j], yn_dev, 3, where != 1)

    def kv_forward(k, where):
        at = kv_all.at[:, z_from[k]]
        arrive(at, sem_kv.at[z_from[k]])
        relay(at, sem_kv.at[z_from[k]], k, where)

    def x_arrive(at_y, slot):
        arrive(xs.at[at_y, slot], sem_x.at[at_y, slot])

    def x_relay(at_y):
        x_arrive(at_y, 2)
        push(xs.at[at_y, 2], xs.at[at_y, 3], sem_x.at[at_y, 3], mate, 2)

    def turn(at_y, slot):
        for j in range(depth // 128):
            at = slice(j * 128, (j + 1) * 128)
            xt[at_y, at, slot * rows : (slot + 1) * rows] = xs[at_y, slot, :, at].T

    def product(j, at_y, first):
        return jnp.dot(
            xs[at_y, first : first + 2].reshape(2 * rows, depth),
            w_all[j, at_y].reshape(depth, chunk),
            preferred_element_type=F32,
        )

    arrive(xs.at[:, 1], sem_x.at[0, 1])
    for slot in range(2):

        @pl.loop(0, 2)
        def _(at_y):
            turn(at_y, slot)

    def spread(slot):
        inv[slot] = jnp.broadcast_to(inv_row[slot, :1], (rows, 128)).T

    for k in range(3):
        forward(0, k)

    @pl.when(mid == 1)
    def _():
        for k in range(3):
            kv_forward(k, 1)

    x_relay(y)
    arrive(inv_row.at[1], sem_inv.at[0])
    spread(1)
    for j in range(2):
        arrive(w_all.at[j, y, pc, z], sem_w.at[j, pc, z])
    pred[0, 0] = product(0, y, 0)
    turn(y, 2)
    x_arrive(y, 3)
    turn(y, 3)
    pred[0, 1] = product(0, y, 2)
    for at in (6, 7, 8):
        ref = (q_ref, len_ref, asg_ref)[at - 6]
        pltpu.make_async_copy((q_hbm, len_hbm, asg_hbm)[at - 6], ref, local_sem.at[at]).wait()

    @pl.when(mid == 1)
    def _():
        for k in range(3):
            forward(1, k, 1)

    @pl.when(mid == 0)
    def _():
        forward(1, 0, 0)
        for k in range(3):
            kv_forward(k, 0)

    ends = []
    total = 0
    for i in range(len_ref.shape[1]):
        total = total + len_ref[0, i]
        ends.append(total)

    def document(position):
        found = jnp.zeros(position.shape, jnp.int32)
        for end in ends:
            found = found + (position >= end).astype(jnp.int32)
        return found

    lanes = lax.broadcasted_iota(jnp.int32, (1, BLK), 1)
    k_pos = jnp.concatenate([asg_ref[0, j] * BLK + lanes for j in range(4)], axis=1)
    q_pos = asg_ref[0, z] * BLK + lax.broadcasted_iota(jnp.int32, (rows, 1), 0)
    allowed = (document(q_pos) == document(k_pos)) & (q_pos >= k_pos)

    def attend(h):
        k_all = kv_all[0].reshape(4 * rows, HD)
        v_all = kv_all[1].reshape(4 * rows, HD)
        scores = lax.dot_general(
            q_ref[:, h * HD : (h + 1) * HD], k_all, (((1,), (1,)), ((), ())),
            preferred_element_type=F32,
        ) * HD ** (-0.5)
        masked = jnp.where(allowed, scores, NEGATIVE)
        top = jnp.max(masked, axis=1, keepdims=True)
        terms = jnp.where(allowed, jnp.exp(masked - top), 0.0)
        totals = jnp.sum(terms, axis=1, keepdims=True)
        mixture = jnp.dot(terms.astype(BF16), v_all, preferred_element_type=F32)
        done = (mixture / totals).astype(BF16)
        att_ref[:, h * HD : (h + 1) * HD] = done
        att_half[h // 2, h % 2] = done

    def part_send(j, slot, value):
        p_out[j, slot] = value.astype(BF16)
        at = (j, (slot + 2) % 4)
        push(p_out.at[j, slot], p_in.at[at], sem_p.at[at], xn_dev, 2)

    def fold(j, slot, attended):
        at = slice(slot * rows, (slot + 1) * rows)
        value = pred[j, 0, at, :] - attended.astype(F32) / inv[slot]
        pred[j, 0, at, :] = value
        part_send(j, slot, value)

    def exchange(j):
        arrive(w_all.at[j, yo], sem_w_far.at[j])
        pred[j, 0] += product(j, yo, 0)
        fold(j, 0, att_half[c, j])
        arrive(att_peer.at[j], sem_att.at[j])
        fold(j, 1, att_peer[j])
        if j == 0:
            x_arrive(yo, 3)
        pred[j, 1] += product(j, yo, 2)
        for slot in range(2):
            part_send(j, 2 + slot, pred[j, 1, slot * rows : (slot + 1) * rows, :])

    attend(0)
    x_relay(yo)
    attend(2)
    push(att_half.at[pc, 0], att_peer.at[0], sem_att.at[0], mate, 2)
    exchange(0)

    @pl.when(mid == 0)
    def _():
        forward(1, 1, 0)
        forward(1, 2, 0)

    attend(1)
    attend(3)
    push(att_half.at[pc, 1], att_peer.at[1], sem_att.at[1], mate, 2)
    pred[1, 0] = product(1, y, 0)
    pred[1, 1] = product(1, y, 2)
    turn(yo, 2)
    turn(yo, 3)
    arrive(inv_row.at[2:4], sem_inv.at[1])
    spread(2)
    spread(3)
    exchange(1)

    def scale_rows(j, slot):
        arrive(p_in.at[j, slot], sem_p.at[j, slot])
        at = slice((slot % 2) * rows, (slot % 2 + 1) * rows)
        factor = inv[slot]
        raw = pred[j, slot // 2, at, :] + p_in[j, slot].astype(F32)
        s_all[j, slot] = (raw * factor * (factor * token_total ** (-0.5))).astype(BF16)

    def grad(j, at_y):
        return jnp.dot(
            xt[at_y], s_all[j].reshape(4 * rows, chunk), preferred_element_type=F32
        ).reshape(2, 4, piece, chunk)

    order = (3, 2, 1, 0)
    for j in range(2):
        for slot in (2, 3, 0, 1):
            scale_rows(j, slot)
        s_y[j] = grad(j, yo).astype(BF16)
        for r in order:
            at = (j, slice(None), zs[r])
            push(s_y.at[at], r_y.at[at], sem_ry.at[j, zs[r]], yn_dev, 4)
        grad_f[j] = grad(j, y)

    def column_sum(j, part, g):
        return grad_f[j, part, g] + r_y[j, part, g].astype(F32)

    def z_push(j, part, g, dev):
        push(s_z.at[j, part, g], r_z.at[j, z, c], sem_rz.at[j], dev, 4)

    for j in range(2):
        for r in order[:3]:
            g = zs[r]
            arrive(r_y.at[j, :, g], sem_ry.at[j, g])
            for part in range(2):
                s_z[j, part, g] = column_sum(j, part, g).astype(BF16)
            z_push(j, c, g, z_dev[r])
            z_push(j, pc, g, z_mate[r])
        arrive(r_y.at[j, :, z], sem_ry.at[j, z])
        for part in range(2):
            grad_f[j, part, z] = column_sum(j, part, z)
        s_z[j, pc, z] = grad_f[j, pc, z].astype(BF16)
        z_push(j, pc, z, mate)
    for j in range(2):
        amount(7 * piece, sem_rz.at[j]).wait()
        total = grad_f[j, c, z]
        for r in range(1, 4):
            total = total + r_z[j, zs[r], c].astype(F32)
        out_ref[:, cols(c, j)] = total
        total = jnp.zeros((piece, chunk), F32)
        for r in (3, 2, 1, 0):
            total = total + r_z[j, zs[r], pc].astype(F32)
        out_ref[:, cols(pc, j)] = total
    for group in range(5):
        amount(sent[group], send.at[group]).wait()
    pl.when(mid == 1)(amount(sum(relayed), send.at[5]).wait)


def local_fused(student_in, weight, queries, keys, values, lengths, assignment):
    rows, width = student_in.shape
    piece, features = weight.shape
    chunk = features // 4
    depth = width // 4
    token_total = rows * lax.axis_size("dp") * lax.axis_size("seq")
    vmem = pl.BlockSpec(memory_space=pltpu.VMEM)
    hbm = pl.BlockSpec(memory_space=pltpu.HBM)
    dma = pltpu.SemaphoreType.DMA
    quarter = (2, 4, piece, chunk)
    return pl.pallas_call(
        functools.partial(fused_kernel, token_total),
        out_shape=(
            pltpu.VMEM((rows, features), BF16),
            pltpu.VMEM((piece, features), F32),
        ),
        in_specs=[hbm] * 7,
        out_specs=(vmem, vmem),
        scratch_shapes=[
            pltpu.VMEM((2, 4, rows, depth), BF16),
            pltpu.VMEM((2, rows, depth), BF16),
            pltpu.VMEM((2, depth, 4 * rows), BF16),
            pltpu.VMEM((2, 2) + quarter, BF16),
            pltpu.VMEM((2, piece, chunk), BF16),
            pltpu.VMEM((rows, features), BF16),
            pltpu.VMEM((2, 4, rows, HD), BF16),
            pltpu.SMEM(lengths.shape, jnp.int32),
            pltpu.SMEM(assignment.shape, jnp.int32),
            pltpu.VMEM((4, rows, 128), F32),
            pltpu.VMEM((4, 8, 128), F32),
            pltpu.VMEM((2, 2, 2 * rows, chunk), F32),
            pltpu.VMEM((2, 4, rows, chunk), BF16),
            pltpu.VMEM((2, 4, rows, chunk), BF16),
            pltpu.VMEM((2, 4, rows, chunk), BF16),
            pltpu.VMEM((2, 2, rows, chunk), BF16),
            pltpu.VMEM((2, rows, chunk), BF16),
            pltpu.VMEM((2,) + quarter, F32),
            pltpu.VMEM((2,) + quarter, BF16),
            pltpu.VMEM((2,) + quarter, BF16),
            pltpu.VMEM((2,) + quarter, BF16),
            pltpu.VMEM((2, 4, 2, piece, chunk), BF16),
            pltpu.VMEM((8192, 128), BF16),
            dma((9,)),
            dma((6,)),
            dma((2, 2, 4)),
            dma((2,)),
            dma((4,)),
            dma((2, 4)),
            dma((2,)),
            dma((2,)),
            dma((2, 4)),
            dma((2, 4)),
            dma((2,)),
        ],
        compiler_params=pltpu.CompilerParams(collective_id=0, has_side_effects=True),
        name="distill",
    )(student_in, weight, queries, keys, values, lengths, assignment)


def fits(student_in, weight, queries, keys, values, lengths, assignment):
    rows, width = student_in.shape
    piece, features = weight.shape
    return (
        lax.axis_size("dp") == 8
        and lax.axis_size("seq") == 4
        and rows == BLK
        and assignment.shape[1] == 4
        and piece % 16 == 0
        and width == 32 * piece
        and width % 512 == 0
        and features == HQ * HD
        and keys.shape[1] == HD
    )


def dispatch(*arrays):
    return local_fused(*arrays) if fits(*arrays) else local(*arrays)


def solution(mesh):
    placed = (
        P(("dp", "seq"), None),
        P(("dp", "seq"), None),
        P(("dp", "seq"), None),
        P(("dp", "seq"), None),
        P(("dp", "seq"), None),
        P("dp", None),
        P("dp", None),
    )
    return jax.shard_map(
        dispatch,
        mesh=mesh,
        in_specs=placed,
        out_specs=(P(("dp", "seq"), None), P(("dp", "seq"), None)),
        check_vma=False,
    )
```

time: 47.8 us -> 42.6 us (0.89)
  Pallas kernels: 44.6 us -> 40.4 us
  local copies, waits for them, and re-layouts: 2.3 us -> 1.35 us
    pallas_call x1, Pallas kernels: 44.6 us -> 40.4 us  [local_fused(): pl.pallas_call(functools.partial(fused_kernel, token_total), out_shape=(p...]
    unnamed x4 -> x2, local copies, waits for them, and re-layouts: 2.3 us -> 1.35 us
where the time goes in v2:
time: 42.6 us; the launch traced here: 42.4 us
  Pallas kernels  40.4 us (95%)
  local copies, waits for them, and re-layouts  1.35 us (3%)
  between operations  0.64 us (2%)
    pallas_call x1, Pallas kernels, local_fused(): pl.pallas_call(functools.partial(fused_kernel, token_total), out_shape=(p...  40.4 us
    unnamed x2, local copies, waits for them, and re-layouts  1.35 us

profile of v2, /device:TPU:0, one launch (start us, length us, event | category | flops | bytes accessed | tf_op | source)
XLA Modules:
  0.0 42.4 jit_solution(7630157132311411387)
XLA Ops:
  0.6 40.4 %distill.1 = (bf16[128,512]{1,0:T(8,128)(2,1)S(1)}, f32[112,512]{1,0:T(8,128)S(1)}) custom-call(bf16[128,3584]{1,0:T(8,128)(2,1)} %x_hbm.1, bf16[112,512]{1,0:T(8,128)(2,1)} %w_hbm.1, bf16[128,512]{1,0:T(8,128)(2,1)} %q_hbm.1, bf16[128,128]{1,0:T(8,128)(2,1)} %k_hbm.1, bf16[128,128]{1,0:T(8,128)(2,1)} %v_hbm.1, s32[1,4]{1,0:T(1,128)} %len_hbm.1, s32[1,4]{1,0:T(1,128)} %asg_hbm.1), custom_call_target="tpu_custom_call" | custom-call | tf_op jit(solution)/shard_map/distill/pallas_call | solution.py:494
  41.1 0.7 %copy.11 = bf16[128,512]{1,0:T(8,128)(2,1)} copy(bf16[128,512]{1,0:T(8,128)(2,1)S(1)} %get-tuple-element.2) | data formatting | bytes 262144
  41.7 0.7 %copy.12 = f32[112,512]{1,0:T(8,128)} copy(f32[112,512]{1,0:T(8,128)S(1)} %get-tuple-element.3) | data formatting | bytes 458752

commit v3 on v2

--- a/solution.py
+++ b/solution.py
@@ -151,8 +151,8 @@
     z_two = mid * zs[3] + (1 - mid) * zs[2]
     z_from = (
         mid * zs[3] + (1 - mid) * zs[1],
-        mid * zs[1] + (1 - mid) * zs[2],
-        mid * zs[2] + (1 - mid) * zs[3],
+        zs[2],
+        mid * zs[1] + (1 - mid) * zs[3],
     )
     z_dev = [(dp, zs[r]) for r in range(4)]
     z_mate = [(dp_m, zs[r]) for r in range(4)]
@@ -216,29 +216,34 @@
             device_id=mate, device_id_type=MESH,
         ).wait_recv()
 
-    def w_start(j):
-        at = (j, y, c, z)
-        dst, sem = w_all.at[at], sem_w.at[j, c, z]
-        amount(get_w[j], local_sem.at[j]).wait()
-        push(dst, dst, sem, (dp, z_two), 0)
-        push(w_peer.at[j], dst, sem, (dp_m, z_two), 0)
-        push(dst, dst, sem, z_dev[1], 0)
-        push(w_peer.at[j], dst, sem, z_mate[1], 0)
+    def w_along(j, to):
+        dst, sem = w_all.at[j, y, c, z], sem_w.at[j, z]
+        push(dst, dst, sem, (dp, to), 0)
+        push(w_peer.at[j], dst, sem, (dp_m, to), 0)
+
+    def w_across(j):
+        dst, sem = w_all.at[j, y, c, z], sem_w.at[j, z]
         push(dst, dst, sem_w_far.at[j], yn_dev, 0)
         push(w_peer.at[j], dst, sem_w_far.at[j], yn_mate, 0)
         push(w_peer.at[j], dst, sem, mate, 0)
 
-    w_start(0)
+    kv_own = kv_all.at[:, z]
+    amount(get_w[0], local_sem.at[0]).wait()
+    w_along(0, z_two)
+    w_along(0, zs[1])
+    w_across(0)
+    amount(get_kv, local_sem.at[4]).wait()
+    push(kv_own, kv_own, sem_kv.at[z], (dp, z_two), 2)
+    push(kv_own, kv_own, sem_kv.at[z], z_dev[1], 2)
     for i, at_y in enumerate((y, yo)):
         amount(get_xo[i], local_sem.at[2 + i]).wait()
-        push(xo.at[at_y], xs.at[at_y, 2], sem_x.at[at_y, 2], xn_dev, 1)
-    amount(get_kv, local_sem.at[4]).wait()
-    kv_own = kv_all.at[:, z]
-    push(kv_own, kv_own, sem_kv.at[z], (dp, z_two), 2)
-    push(kv_own, kv_own, sem_kv.at[z], z_dev[1], 2)
-    w_start(1)
+        push(xo.at[at_y], xs.at[at_y, 2], sem_x.at[at_y, 0], xn_dev, 1)
+    amount(get_w[1], local_sem.at[1]).wait()
+    w_along(1, z_two)
+    w_along(1, zs[1])
+    w_across(1)
     amount(get_xs, local_sem.at[5]).wait()
-    push(xs.at[:, 0], xs.at[:, 1], sem_x.at[0, 1], mate, 1)
+    push(xs.at[:, 0], xs.at[:, 1], sem_x.at[0, 2], mate, 1)
 
     step = 16
 
@@ -260,7 +265,7 @@
     relayed = []
 
     def relay(ref, sem, k, where):
-        if k == 1 or where == 0:
+        if k == 2 or where == 0:
             return
         copy = pltpu.make_async_remote_copy(
             src_ref=ref, dst_ref=ref, send_sem=send.at[5], recv_sem=sem,
@@ -273,11 +278,10 @@
         relayed.append(lines(ref))
 
     def forward(j, k, where=None):
-        for part in range(2):
-            at = (j, y, part, z_from[k])
-            arrive(w_all.at[at], sem_w.at[j, part, z_from[k]])
-            relay(w_all.at[at], sem_w.at[j, part, z_from[k]], k, where)
-            push(w_all.at[at], w_all.at[at], sem_w_far.at[j], yn_dev, 3, where != 1)
+        at = w_all.at[j, y, :, z_from[k]]
+        arrive(at, sem_w.at[j, z_from[k]])
+        relay(at, sem_w.at[j, z_from[k]], k, where)
+        push(at, at, sem_w_far.at[j], yn_dev, 3, where != 1)
 
     def kv_forward(k, where):
         at = kv_all.at[:, z_from[k]]
@@ -285,11 +289,11 @@
         relay(at, sem_kv.at[z_from[k]], k, where)
 
     def x_arrive(at_y, slot):
-        arrive(xs.at[at_y, slot], sem_x.at[at_y, slot])
+        arrive(xs.at[at_y, slot], sem_x.at[at_y, slot - 2])
 
     def x_relay(at_y):
         x_arrive(at_y, 2)
-        push(xs.at[at_y, 2], xs.at[at_y, 3], sem_x.at[at_y, 3], mate, 2)
+        push(xs.at[at_y, 2], xs.at[at_y, 3], sem_x.at[at_y, 1], mate, 2)
 
     def turn(at_y, slot):
         for j in range(depth // 128):
@@ -303,7 +307,7 @@
             preferred_element_type=F32,
         )
 
-    arrive(xs.at[:, 1], sem_x.at[0, 1])
+    arrive(xs.at[:, 1], sem_x.at[0, 2])
     for slot in range(2):
 
         @pl.loop(0, 2)
@@ -315,6 +319,9 @@
 
     for k in range(3):
         forward(0, k)
+    for j in range(2):
+        arrive(w_all.at[j, y, pc, z], sem_w.at[j, z])
+    pred[0, 0] = product(0, y, 0)
 
     @pl.when(mid == 1)
     def _():
@@ -324,24 +331,19 @@
     x_relay(y)
     arrive(inv_row.at[1], sem_inv.at[0])
     spread(1)
-    for j in range(2):
-        arrive(w_all.at[j, y, pc, z], sem_w.at[j, pc, z])
-    pred[0, 0] = product(0, y, 0)
-    turn(y, 2)
-    x_arrive(y, 3)
-    turn(y, 3)
-    pred[0, 1] = product(0, y, 2)
     for at in (6, 7, 8):
         ref = (q_ref, len_ref, asg_ref)[at - 6]
         pltpu.make_async_copy((q_hbm, len_hbm, asg_hbm)[at - 6], ref, local_sem.at[at]).wait()
 
-    @pl.when(mid == 1)
-    def _():
-        for k in range(3):
-            forward(1, k, 1)
+    def near_rows():
+        turn(y, 2)
+        x_arrive(y, 3)
+        turn(y, 3)
+        pred[0, 1] = product(0, y, 2)
 
     @pl.when(mid == 0)
     def _():
+        near_rows()
         forward(1, 0, 0)
         for k in range(3):
             kv_forward(k, 0)
@@ -390,29 +392,41 @@
         pred[j, 0, at, :] = value
         part_send(j, slot, value)
 
-    def exchange(j):
+    def fold_first(j):
         arrive(w_all.at[j, yo], sem_w_far.at[j])
         pred[j, 0] += product(j, yo, 0)
         fold(j, 0, att_half[c, j])
+
+    def fold_second(j):
         arrive(att_peer.at[j], sem_att.at[j])
         fold(j, 1, att_peer[j])
-        if j == 0:
-            x_arrive(yo, 3)
-        pred[j, 1] += product(j, yo, 2)
-        for slot in range(2):
-            part_send(j, 2 + slot, pred[j, 1, slot * rows : (slot + 1) * rows, :])
+
+    def far_rows(j, slot):
+        at = slice(slot * rows, (slot + 1) * rows)
+        value = pred[j, 1, at, :] + jnp.dot(
+            xs[yo, 2 + slot], w_all[j, yo].reshape(depth, chunk), preferred_element_type=F32
+        )
+        pred[j, 1, at, :] = value
+        part_send(j, 2 + slot, value)
 
     attend(0)
-    x_relay(yo)
     attend(2)
     push(att_half.at[pc, 0], att_peer.at[0], sem_att.at[0], mate, 2)
-    exchange(0)
-
-    @pl.when(mid == 0)
+
+    @pl.when(mid == 1)
     def _():
-        forward(1, 1, 0)
-        forward(1, 2, 0)
-
+        near_rows()
+        for k in range(3):
+            forward(1, k, 1)
+
+    fold_first(0)
+    x_relay(yo)
+    pl.when(mid == 0)(functools.partial(forward, 1, 1, 0))
+    fold_second(0)
+    far_rows(0, 0)
+    x_arrive(yo, 3)
+    far_rows(0, 1)
+    pl.when(mid == 0)(functools.partial(forward, 1, 2, 0))
     attend(1)
     attend(3)
     push(att_half.at[pc, 1], att_peer.at[1], sem_att.at[1], mate, 2)
@@ -423,7 +437,10 @@
     arrive(inv_row.at[2:4], sem_inv.at[1])
     spread(2)
     spread(3)
-    exchange(1)
+    fold_first(1)
+    fold_second(1)
+    far_rows(1, 0)
+    far_rows(1, 1)
 
     def scale_rows(j, slot):
         arrive(p_in.at[j, slot], sem_p.at[j, slot])
@@ -441,10 +458,21 @@
     for j in range(2):
         for slot in (2, 3, 0, 1):
             scale_rows(j, slot)
-        s_y[j] = grad(j, yo).astype(BF16)
-        for r in order:
-            at = (j, slice(None), zs[r])
-            push(s_y.at[at], r_y.at[at], sem_ry.at[j, zs[r]], yn_dev, 4)
+        for near in range(2):
+            first = 2 * ((z // 2 + 1 + near) % 2)
+            for part in range(2):
+                lead = pl.multiple_of((part * 4 + first) * piece, 16)
+                s_y[j, part, pl.ds(first, 2)] = jnp.dot(
+                    xt[yo, pl.ds(lead, 2 * piece), :], s_all[j].reshape(4 * rows, chunk),
+                    preferred_element_type=F32,
+                ).astype(BF16).reshape(2, piece, chunk)
+            if j == 0:
+                at = (j, slice(None), pl.ds(first, 2))
+                push(s_y.at[at], r_y.at[at], sem_ry.at[j, near], yn_dev, 4)
+            else:
+                for r in ((3, 2), (1, 0))[near]:
+                    at = (j, slice(None), zs[r])
+                    push(s_y.at[at], r_y.at[at], sem_ry.at[j, r], yn_dev, 4)
         grad_f[j] = grad(j, y)
 
     def column_sum(j, part, g):
@@ -454,14 +482,18 @@
         push(s_z.at[j, part, g], r_z.at[j, z, c], sem_rz.at[j], dev, 4)
 
     for j in range(2):
-        for r in order[:3]:
+        for r in order:
             g = zs[r]
-            arrive(r_y.at[j, :, g], sem_ry.at[j, g])
-            for part in range(2):
-                s_z[j, part, g] = column_sum(j, part, g).astype(BF16)
-            z_push(j, c, g, z_dev[r])
-            z_push(j, pc, g, z_mate[r])
-        arrive(r_y.at[j, :, z], sem_ry.at[j, z])
+            if j == 1:
+                arrive(r_y.at[j, :, g], sem_ry.at[j, r])
+            elif r % 2:
+                first = 2 * ((z // 2 + 1 + (3 - r) // 2) % 2)
+                arrive(r_y.at[j, :, pl.ds(first, 2)], sem_ry.at[j, (3 - r) // 2])
+            if r:
+                for part in range(2):
+                    s_z[j, part, g] = column_sum(j, part, g).astype(BF16)
+                z_push(j, c, g, z_dev[r])
+                z_push(j, pc, g, z_mate[r])
         for part in range(2):
             grad_f[j, part, z] = column_sum(j, part, z)
         s_z[j, pc, z] = grad_f[j, pc, z].astype(BF16)
@@ -481,6 +513,17 @@
     pl.when(mid == 1)(amount(sum(relayed), send.at[5]).wait)
 
 
+def put_kernel(att_ref, grad_ref, att_out, grad_out, sem):
+    copies = [
+        pltpu.make_async_copy(att_ref, att_out, sem.at[0]),
+        pltpu.make_async_copy(grad_ref, grad_out, sem.at[1]),
+    ]
+    for copy in copies:
+        copy.start()
+    for copy in copies:
+        copy.wait()
+
+
 def local_fused(student_in, weight, queries, keys, values, lengths, assignment):
     rows, width = student_in.shape
     piece, features = weight.shape
@@ -491,7 +534,7 @@
     hbm = pl.BlockSpec(memory_space=pltpu.HBM)
     dma = pltpu.SemaphoreType.DMA
     quarter = (2, 4, piece, chunk)
-    return pl.pallas_call(
+    held = pl.pallas_call(
         functools.partial(fused_kernel, token_total),
         out_shape=(
             pltpu.VMEM((rows, features), BF16),
@@ -525,10 +568,10 @@
             pltpu.VMEM((8192, 128), BF16),
             dma((9,)),
             dma((6,)),
-            dma((2, 2, 4)),
+            dma((2, 4)),
             dma((2,)),
             dma((4,)),
-            dma((2, 4)),
+            dma((2, 3)),
             dma((2,)),
             dma((2,)),
             dma((2, 4)),
@@ -538,6 +581,17 @@
         compiler_params=pltpu.CompilerParams(collective_id=0, has_side_effects=True),
         name="distill",
     )(student_in, weight, queries, keys, values, lengths, assignment)
+    return pl.pallas_call(
+        put_kernel,
+        out_shape=(
+            jax.ShapeDtypeStruct((rows, features), BF16),
+            jax.ShapeDtypeStruct((piece, features), F32),
+        ),
+        in_specs=[vmem] * 2,
+        out_specs=(hbm, hbm),
+        scratch_shapes=[dma((2,))],
+        name="put",
+    )(*(pltpu.with_memory_space_constraint(h, pltpu.VMEM) for h in held))
 
 
 def fits(student_in, weight, queries, keys, values, lengths, assignment):

time: 42.6 us -> 39.7 us (0.932)
  Pallas kernels: 40.4 us -> 38.9 us
  local copies, waits for them, and re-layouts: 1.35 us -> 0 us
    pallas_call x1, Pallas kernels: 40.4 us -> 38.2 us  [local_fused(): pl.pallas_call(functools.partial(fused_kernel, token_total), out_shape=(p...]
    unnamed x2 -> x0, local copies, waits for them, and re-layouts: 1.35 us -> none
    pallas_call x0 -> x1, Pallas kernels: none -> 0.75 us  [local_fused(): pl.pallas_call(put_kernel, out_shape=(jax.ShapeDtypeStruct((rows, feature...]
where the time goes in v3:
time: 39.7 us; the launch traced here: 39.6 us
  Pallas kernels  38.9 us (98%)
  between operations  0.64 us (2%)
    pallas_call x1, Pallas kernels, local_fused(): pl.pallas_call(functools.partial(fused_kernel, token_total), out_shape=(p...  38.2 us

profile of v3, /device:TPU:0, one launch (start us, length us, event | category | flops | bytes accessed | tf_op | source)
XLA Modules:
  0.0 39.6 jit_solution(17399634119155683102)
XLA Ops:
  0.6 38.2 %distill.1 = (bf16[128,512]{1,0:T(8,128)(2,1)S(1)}, f32[112,512]{1,0:T(8,128)S(1)}) custom-call(bf16[128,3584]{1,0:T(8,128)(2,1)} %x_hbm.1, bf16[112,512]{1,0:T(8,128)(2,1)} %w_hbm.1, bf16[128,512]{1,0:T(8,128)(2,1)} %q_hbm.1, bf16[128,128]{1,0:T(8,128)(2,1)} %k_hbm.1, bf16[128,128]{1,0:T(8,128)(2,1)} %v_hbm.1, s32[1,4]{1,0:T(1,128)} %len_hbm.1, s32[1,4]{1,0:T(1,128)} %asg_hbm.1), custom_call_target="tpu_custom_call" | custom-call | tf_op jit(solution)/shard_map/distill/pallas_call | solution.py:537
  38.8 0.8 %put.1 = (bf16[128,512]{1,0:T(8,128)(2,1)}, f32[112,512]{1,0:T(8,128)}) custom-call(bf16[128,512]{1,0:T(8,128)(2,1)S(1)} %get-tuple-element.4.att_ref, f32[112,512]{1,0:T(8,128)S(1)} %get-tuple-element.5.grad_ref), custom_call_target="tpu_custom_call" | custom-call | tf_op jit(solution)/shard_map/put/pallas_call | solution.py:584

commit v4 on v3

--- a/solution.py
+++ b/solution.py
@@ -190,25 +190,25 @@
         for j in range(2)
     ]
     get_xo = [
-        fetch(2 + i, (x_hbm.at[:, width(at, 1 - x)], xo.at[at])) for i, at in enumerate((y, yo))
+        fetch(1, (x_hbm.at[:, width(at, 1 - x)], xo.at[at])) for i, at in enumerate((y, yo))
     ]
-    get_kv = fetch(4, *((ref, kv_all.at[i, z]) for i, ref in enumerate((k_hbm, v_hbm))))
-    get_xs = fetch(5, *((x_hbm.at[:, width(at, x)], xs.at[at, 0]) for at in (y, yo)))
-    fetch(6, (q_hbm, q_ref))
-    fetch(7, (len_hbm, len_ref))
-    fetch(8, (asg_hbm, asg_ref))
+    get_kv = fetch(1, *((ref, kv_all.at[i, z]) for i, ref in enumerate((k_hbm, v_hbm))))
+    get_xs = fetch(1, *((x_hbm.at[:, width(at, x)], xs.at[at, 0]) for at in (y, yo)))
+    get_q = fetch(1, (q_hbm, q_ref))
+    fetch(2, (len_hbm, len_ref))
+    fetch(3, (asg_hbm, asg_ref))
     pl.semaphore_wait(barrier, len(greeted))
 
-    sent = [0, 0, 0, 0, 0]
+    sent = [0, 0, 0]
 
     def push(src, dst, rsem, dev, group, counted=True):
         copy = pltpu.make_async_remote_copy(
-            src_ref=src, dst_ref=dst, send_sem=send.at[group], recv_sem=rsem,
+            src_ref=src, dst_ref=dst, send_sem=send.at[(0, 1, 1, 0, 2)[group]], recv_sem=rsem,
             device_id=dev, device_id_type=MESH,
         )
         copy.start()
         if counted:
-            sent[group] += lines(src)
+            sent[(0, 1, 1, 0, 2)[group]] += lines(src)
 
     def arrive(dst, rsem):
         pltpu.make_async_remote_copy(
@@ -232,18 +232,15 @@
     w_along(0, z_two)
     w_along(0, zs[1])
     w_across(0)
-    amount(get_kv, local_sem.at[4]).wait()
+    amount(get_w[1] + sum(get_xo) + get_kv + get_xs + get_q, local_sem.at[1]).wait()
     push(kv_own, kv_own, sem_kv.at[z], (dp, z_two), 2)
     push(kv_own, kv_own, sem_kv.at[z], z_dev[1], 2)
-    for i, at_y in enumerate((y, yo)):
-        amount(get_xo[i], local_sem.at[2 + i]).wait()
-        push(xo.at[at_y], xs.at[at_y, 2], sem_x.at[at_y, 0], xn_dev, 1)
-    amount(get_w[1], local_sem.at[1]).wait()
+    for at_y in (y, yo):
+        push(xo.at[at_y], xs.at[at_y, 2], sem_x.at[2 * at_y], xn_dev, 1)
     w_along(1, z_two)
     w_along(1, zs[1])
     w_across(1)
-    amount(get_xs, local_sem.at[5]).wait()
-    push(xs.at[:, 0], xs.at[:, 1], sem_x.at[0, 2], mate, 1)
+    push(xs.at[:, 0], xs.at[:, 1], sem_x.at[4], mate, 1)
 
     step = 16
 
@@ -268,7 +265,7 @@
         if k == 2 or where == 0:
             return
         copy = pltpu.make_async_remote_copy(
-            src_ref=ref, dst_ref=ref, send_sem=send.at[5], recv_sem=sem,
+            src_ref=ref, dst_ref=ref, send_sem=send.at[3], recv_sem=sem,
             device_id=z_dev[1], device_id_type=MESH,
         )
         if where == 1:
@@ -289,11 +286,11 @@
         relay(at, sem_kv.at[z_from[k]], k, where)
 
     def x_arrive(at_y, slot):
-        arrive(xs.at[at_y, slot], sem_x.at[at_y, slot - 2])
+        arrive(xs.at[at_y, slot], sem_x.at[2 * at_y + slot - 2])
 
     def x_relay(at_y):
         x_arrive(at_y, 2)
-        push(xs.at[at_y, 2], xs.at[at_y, 3], sem_x.at[at_y, 1], mate, 2)
+        push(xs.at[at_y, 2], xs.at[at_y, 3], sem_x.at[2 * at_y + 1], mate, 2)
 
     def turn(at_y, slot):
         for j in range(depth // 128):
@@ -307,7 +304,7 @@
             preferred_element_type=F32,
         )
 
-    arrive(xs.at[:, 1], sem_x.at[0, 2])
+    arrive(xs.at[:, 1], sem_x.at[4])
     for slot in range(2):
 
         @pl.loop(0, 2)
@@ -331,9 +328,8 @@
     x_relay(y)
     arrive(inv_row.at[1], sem_inv.at[0])
     spread(1)
-    for at in (6, 7, 8):
-        ref = (q_ref, len_ref, asg_ref)[at - 6]
-        pltpu.make_async_copy((q_hbm, len_hbm, asg_hbm)[at - 6], ref, local_sem.at[at]).wait()
+    pltpu.make_async_copy(len_hbm, len_ref, local_sem.at[2]).wait()
+    pltpu.make_async_copy(asg_hbm, asg_ref, local_sem.at[3]).wait()
 
     def near_rows():
         turn(y, 2)
@@ -384,7 +380,7 @@
     def part_send(j, slot, value):
         p_out[j, slot] = value.astype(BF16)
         at = (j, (slot + 2) % 4)
-        push(p_out.at[j, slot], p_in.at[at], sem_p.at[at], xn_dev, 2)
+        push(p_out.at[j, slot], p_in.at[at], sem_p.at[j * (1 + at[1])], xn_dev, 2)
 
     def fold(j, slot, attended):
         at = slice(slot * rows, (slot + 1) * rows)
@@ -443,7 +439,10 @@
     far_rows(1, 1)
 
     def scale_rows(j, slot):
-        arrive(p_in.at[j, slot], sem_p.at[j, slot])
+        if j == 1:
+            arrive(p_in.at[j, slot], sem_p.at[1 + slot])
+        elif slot == 2:
+            arrive(p_in.at[j], sem_p.at[0])
         at = slice((slot % 2) * rows, (slot % 2 + 1) * rows)
         factor = inv[slot]
         raw = pred[j, slot // 2, at, :] + p_in[j, slot].astype(F32)
@@ -468,11 +467,11 @@
                 ).astype(BF16).reshape(2, piece, chunk)
             if j == 0:
                 at = (j, slice(None), pl.ds(first, 2))
-                push(s_y.at[at], r_y.at[at], sem_ry.at[j, near], yn_dev, 4)
+                push(s_y.at[at], r_y.at[at], sem_ry.at[near], yn_dev, 4)
             else:
                 for r in ((3, 2), (1, 0))[near]:
                     at = (j, slice(None), zs[r])
-                    push(s_y.at[at], r_y.at[at], sem_ry.at[j, r], yn_dev, 4)
+                    push(s_y.at[at], r_y.at[at], sem_ry.at[2 + r], yn_dev, 4)
         grad_f[j] = grad(j, y)
 
     def column_sum(j, part, g):
@@ -485,10 +484,10 @@
         for r in order:
             g = zs[r]
             if j == 1:
-                arrive(r_y.at[j, :, g], sem_ry.at[j, r])
+                arrive(r_y.at[j, :, g], sem_ry.at[2 + r])
             elif r % 2:
                 first = 2 * ((z // 2 + 1 + (3 - r) // 2) % 2)
-                arrive(r_y.at[j, :, pl.ds(first, 2)], sem_ry.at[j, (3 - r) // 2])
+                arrive(r_y.at[j, :, pl.ds(first, 2)], sem_ry.at[(3 - r) // 2])
             if r:
                 for part in range(2):
                     s_z[j, part, g] = column_sum(j, part, g).astype(BF16)
@@ -508,9 +507,9 @@
         for r in (3, 2, 1, 0):
             total = total + r_z[j, zs[r], pc].astype(F32)
         out_ref[:, cols(pc, j)] = total
-    for group in range(5):
+    for group in range(3):
         amount(sent[group], send.at[group]).wait()
-    pl.when(mid == 1)(amount(sum(relayed), send.at[5]).wait)
+    pl.when(mid == 1)(amount(sum(relayed), send.at[3]).wait)
 
 
 def put_kernel(att_ref, grad_ref, att_out, grad_out, sem):
@@ -566,16 +565,16 @@
             pltpu.VMEM((2,) + quarter, BF16),
             pltpu.VMEM((2, 4, 2, piece, chunk), BF16),
             pltpu.VMEM((8192, 128), BF16),
-            dma((9,)),
-            dma((6,)),
+            dma((4,)),
+            dma((4,)),
             dma((2, 4)),
             dma((2,)),
             dma((4,)),
-            dma((2, 3)),
+            dma((5,)),
             dma((2,)),
             dma((2,)),
-            dma((2, 4)),
-            dma((2, 4)),
+            dma((5,)),
+            dma((6,)),
             dma((2,)),
         ],
         compiler_params=pltpu.CompilerParams(collective_id=0, has_side_effects=True),

time: 39.7 us -> 39.6 us (level)
  no operation moved by 1% of the time
where the time goes in v4:
time: 39.6 us; the launch traced here: 39.4 us
  Pallas kernels  38.8 us (98%)
  between operations  0.64 us (2%)
    pallas_call x1, Pallas kernels, local_fused(): pl.pallas_call(functools.partial(fused_kernel, token_total), out_shape=(p...  38 us

profile of v4, /device:TPU:0, one launch (start us, length us, event | category | flops | bytes accessed | tf_op | source)
XLA Modules:
  0.0 39.4 jit_solution(1763738186359973278)
XLA Ops:
  0.6 38.0 %distill.1 = (bf16[128,512]{1,0:T(8,128)(2,1)S(1)}, f32[112,512]{1,0:T(8,128)S(1)}) custom-call(bf16[128,3584]{1,0:T(8,128)(2,1)} %x_hbm.1, bf16[112,512]{1,0:T(8,128)(2,1)} %w_hbm.1, bf16[128,512]{1,0:T(8,128)(2,1)} %q_hbm.1, bf16[128,128]{1,0:T(8,128)(2,1)} %k_hbm.1, bf16[128,128]{1,0:T(8,128)(2,1)} %v_hbm.1, s32[1,4]{1,0:T(1,128)} %len_hbm.1, s32[1,4]{1,0:T(1,128)} %asg_hbm.1), custom_call_target="tpu_custom_call" | custom-call | tf_op jit(solution)/shard_map/distill/pallas_call | solution.py:536
  38.7 0.8 %put.1 = (bf16[128,512]{1,0:T(8,128)(2,1)}, f32[112,512]{1,0:T(8,128)}) custom-call(bf16[128,512]{1,0:T(8,128)(2,1)S(1)} %get-tuple-element.4.att_ref, f32[112,512]{1,0:T(8,128)S(1)} %get-tuple-element.5.grad_ref), custom_call_target="tpu_custom_call" | custom-call | tf_op jit(solution)/shard_map/put/pallas_call | solution.py:583
